TPU v7x, 32 devices: a whole 2x2x4 slice. The times are simulated.
32 devices in a mesh: row: 8 (over y, x, core), col: 4 (over z).
Axes of the slice: x: 2, y: 2, z: 4, core: 2. Of those that a mesh axis runs over, the one named last changes fastest.
Arguments:
- features: bfloat16 [16384, 256], P(('row', 'col')), may hold values from -1 to 3
- in_degree: int32 [16384], P(('row', 'col')), may hold values from 512 to 2047
- tile_index: int32 [8192, 2], P(('row', 'col')), may hold values from 0 to 31, as said below
- tile_count: int32 [32], P(('row', 'col')), may hold values from 1 to 256, as said below
- adjacency_tiles: bfloat16 [8192, 128, 128], P(('row', 'col')), may hold values from 0 to 1, as said below
- projection: bfloat16 [512, 256], replicated, may hold values from -0.25 to 0.25
- out_bias: float32 [256], replicated, may hold values from -3 to 3
Outputs:
- hidden_out: bfloat16 [16384, 256], P(('row', 'col'))
Inputs may be any that keep to these rules, and one draw needn't show every extreme that they name: `tile_index`: column 0 is a local row block below 16, column 1 a local column block below 32, in every slot. `tile_count`: slots at or beyond the count hold tiles and indices that must be ignored; some device has all 256 slots live in every draw. `adjacency_tiles`: entries are 0 or 1.
All inputs are finite; a program needn't handle non-finite values.
Results may differ from a plain program's by a relative error of at most 0.0034.
Values may be sent and summed in bfloat16 or wider, within the bound.
A program may use at most 128 MiB of HBM per device.

v0:
```python
import jax
import jax.numpy as jnp
from jax import lax
from jax.sharding import PartitionSpec as P

BLK = 32


def block_terms(running, col_blocks, index_block, tile_block, live_block):
    picked = col_blocks[index_block[:, 1]]
    kept = jnp.where(live_block[:, None, None], tile_block, jnp.zeros_like(tile_block))
    product = jnp.einsum("kij,kjf->kif", kept, picked, preferred_element_type=jnp.float32)
    flattened = product.reshape(product.shape[0], -1)
    return running.at[index_block[:, 0]].add(flattened)


def local(features, in_degree, tile_index, tile_count, adjacency_tiles, projection, out_bias):
    feat_width = features.shape[1]
    tile_size = adjacency_tiles.shape[1]
    slot_total = adjacency_tiles.shape[0]
    gathered = lax.all_gather(features, "row", axis=0, tiled=True)
    col_blocks = gathered.reshape(gathered.shape[0] // tile_size, tile_size, feat_width)
    row_blocks = features.shape[0] * lax.axis_size("col") // tile_size
    live_count = tile_count[0]
    zeroed = jnp.zeros((row_blocks, tile_size * feat_width), jnp.float32)

    def one_step(running, offset):
        index_block = lax.dynamic_slice_in_dim(tile_index, offset, BLK, 0)
        tile_block = lax.dynamic_slice_in_dim(adjacency_tiles, offset, BLK, 0)
        live_block = offset + jnp.arange(BLK, dtype=jnp.int32) < live_count
        return (block_terms(running, col_blocks, index_block, tile_block, live_block), None)

    summed, _ = lax.scan(one_step, zeroed, jnp.arange(0, slot_total, BLK, dtype=jnp.int32))
    partial_value = summed.reshape(row_blocks * tile_size, feat_width)
    own_sums = lax.psum_scatter(partial_value, "col", scatter_dimension=0, tiled=True)
    neighbour_mean = (own_sums / in_degree[:, None].astype(jnp.float32)).astype(jnp.bfloat16)
    joined = jnp.concatenate([features, neighbour_mean], axis=1)
    mixed = jnp.dot(joined, projection, preferred_element_type=jnp.float32) + out_bias[None, :]
    return jnp.maximum(mixed, 0.0).astype(jnp.bfloat16)


def solution(mesh):
    return jax.shard_map(
        local,
        mesh=mesh,
        in_specs=(
            P(("row", "col"), None),
            P(("row", "col")),
            P(("row", "col"), None),
            P(("row", "col")),
            P(("row", "col"), None, None),
            P(),
            P(),
        ),
        out_specs=P(("row", "col"), None),
        check_vma=False,
    )
```

profile of v0, /device:TPU:0, one launch (start us, length us, event | category | flops | bytes accessed | tf_op | source)
XLA Modules:
  0.0 272.5 jit_solution(9755557317256504715)
XLA Ops:
  7.3 32.4 %all-gather.2.cloned.1.call-done = bf16[4096,256]{1,0:T(8,128)(2,1)} async-done(((bf16[512,256]{1,0:T(8,128)(2,1)}), bf16[4096,256]{1,0:T(8,128)(2,1)}) %all-gather.2.cloned.1.call-update) | async-done | bytes 2097168 | tf_op jit(solution)/shard_map/all_gather | solution.py:21
  39.9 178.2 %while.10 = (s32[]{:T(128)}, f32[16,32768]{1,0:T(8,128)S(1)}, s32[8]{0:T(128)S(1)}, s32[256,2]{0,1:T(2,128)S(1)}, s32[]{:T(128)}, /*index=5*/bf16[256,128,128]{2...) while((s32[]{:T(128)}, f32[16,32768]{1,0:T(8,128)S(1)}, s32[8]{0:T(128)S(1)}, ...), condition=%wide.region_2.3_spmd, body=%wide.region_0.2_spmd.sunk | while | flops 270009600 | bytes 32511596 | solution.py:33
  42.7 3.6 %gather_fusion = bf16[32,128,256]{2,1,0:T(8,128)(2,1)} fusion(bf16[32,128,256]{2,1,0:T(8,128)(2,1)} %get-tuple-element.132, s32[1024]{0:T(1024)S(1)} %pad_clamp_fusion.2), kind=kCustom, calls=%fused_computation.clone.1 | custom fusion | bytes 4194432 | tf_op jit(solution)/shard_map/while/body/eval_jaxpr/gather | solution.py:10
  50.4 4.4 %copy.10 = f32[4,8,128,256]{3,1,2,0:T(8,128)} copy(f32[4,8,128,256]{3,2,1,0:T(8,128)S(1)} %bitcast.21) | data formatting | bytes 8388608 | tf_op jit(solution)/shard_map/while
  54.7 7.4 %scatter_fusion = f32[16,32768]{1,0:T(8,128)S(1)} fusion(f32[16,32768]{1,0:T(8,128)S(1)} %get-tuple-element.117, s32[32]{0:T(128)S(1)} %get-tuple-element.104, f32[32,32768]{1,0:T(8,128)} %bitcast.22), kind=kCustom, calls=%fused_computation.1.clone.1 | custom fusion | flops 1048576 | bytes 12583040 | tf_op jit(solution)/shard_map/while/body/eval_jaxpr/scatter-add | solution.py:14
  65.0 3.6 %gather_fusion = bf16[32,128,256]{2,1,0:T(8,128)(2,1)} fusion(bf16[32,128,256]{2,1,0:T(8,128)(2,1)} %get-tuple-element.132, s32[1024]{0:T(1024)S(1)} %pad_clamp_fusion.2), kind=kCustom, calls=%fused_computation.clone.1 | custom fusion | bytes 4194432 | tf_op jit(solution)/shard_map/while/body/eval_jaxpr/gather | solution.py:10
  72.6 4.4 %copy.10 = f32[4,8,128,256]{3,1,2,0:T(8,128)} copy(f32[4,8,128,256]{3,2,1,0:T(8,128)S(1)} %bitcast.21) | data formatting | bytes 8388608 | tf_op jit(solution)/shard_map/while
  77.0 7.4 %scatter_fusion = f32[16,32768]{1,0:T(8,128)S(1)} fusion(f32[16,32768]{1,0:T(8,128)S(1)} %get-tuple-element.117, s32[32]{0:T(128)S(1)} %get-tuple-element.104, f32[32,32768]{1,0:T(8,128)} %bitcast.22), kind=kCustom, calls=%fused_computation.1.clone.1 | custom fusion | flops 1048576 | bytes 12583040 | tf_op jit(solution)/shard_map/while/body/eval_jaxpr/scatter-add | solution.py:14
  87.3 3.6 %gather_fusion = bf16[32,128,256]{2,1,0:T(8,128)(2,1)} fusion(bf16[32,128,256]{2,1,0:T(8,128)(2,1)} %get-tuple-element.132, s32[1024]{0:T(1024)S(1)} %pad_clamp_fusion.2), kind=kCustom, calls=%fused_computation.clone.1 | custom fusion | bytes 4194432 | tf_op jit(solution)/shard_map/while/body/eval_jaxpr/gather | solution.py:10
  94.9 4.4 %copy.10 = f32[4,8,128,256]{3,1,2,0:T(8,128)} copy(f32[4,8,128,256]{3,2,1,0:T(8,128)S(1)} %bitcast.21) | data formatting | bytes 8388608 | tf_op jit(solution)/shard_map/while
  99.3 7.4 %scatter_fusion = f32[16,32768]{1,0:T(8,128)S(1)} fusion(f32[16,32768]{1,0:T(8,128)S(1)} %get-tuple-element.117, s32[32]{0:T(128)S(1)} %get-tuple-element.104, f32[32,32768]{1,0:T(8,128)} %bitcast.22), kind=kCustom, calls=%fused_computation.1.clone.1 | custom fusion | flops 1048576 | bytes 12583040 | tf_op jit(solution)/shard_map/while/body/eval_jaxpr/scatter-add | solution.py:14
  109.5 3.6 %gather_fusion = bf16[32,128,256]{2,1,0:T(8,128)(2,1)} fusion(bf16[32,128,256]{2,1,0:T(8,128)(2,1)} %get-tuple-element.132, s32[1024]{0:T(1024)S(1)} %pad_clamp_fusion.2), kind=kCustom, calls=%fused_computation.clone.1 | custom fusion | bytes 4194432 | tf_op jit(solution)/shard_map/while/body/eval_jaxpr/gather | solution.py:10
  117.2 4.4 %copy.10 = f32[4,8,128,256]{3,1,2,0:T(8,128)} copy(f32[4,8,128,256]{3,2,1,0:T(8,128)S(1)} %bitcast.21) | data formatting | bytes 8388608 | tf_op jit(solution)/shard_map/while
  121.5 7.4 %scatter_fusion = f32[16,32768]{1,0:T(8,128)S(1)} fusion(f32[16,32768]{1,0:T(8,128)S(1)} %get-tuple-element.117, s32[32]{0:T(128)S(1)} %get-tuple-element.104, f32[32,32768]{1,0:T(8,128)} %bitcast.22), kind=kCustom, calls=%fused_computation.1.clone.1 | custom fusion | flops 1048576 | bytes 12583040 | tf_op jit(solution)/shard_map/while/body/eval_jaxpr/scatter-add | solution.py:14
  139.4 4.4 %copy.10 = f32[4,8,128,256]{3,1,2,0:T(8,128)} copy(f32[4,8,128,256]{3,2,1,0:T(8,128)S(1)} %bitcast.21) | data formatting | bytes 8388608 | tf_op jit(solution)/shard_map/while
  143.8 7.4 %scatter_fusion = f32[16,32768]{1,0:T(8,128)S(1)} fusion(f32[16,32768]{1,0:T(8,128)S(1)} %get-tuple-element.117, s32[32]{0:T(128)S(1)} %get-tuple-element.104, f32[32,32768]{1,0:T(8,128)} %bitcast.22), kind=kCustom, calls=%fused_computation.1.clone.1 | custom fusion | flops 1048576 | bytes 12583040 | tf_op jit(solution)/shard_map/while/body/eval_jaxpr/scatter-add | solution.py:14
  154.1 3.6 %gather_fusion = bf16[32,128,256]{2,1,0:T(8,128)(2,1)} fusion(bf16[32,128,256]{2,1,0:T(8,128)(2,1)} %get-tuple-element.132, s32[1024]{0:T(1024)S(1)} %pad_clamp_fusion.2), kind=kCustom, calls=%fused_computation.clone.1 | custom fusion | bytes 4194432 | tf_op jit(solution)/shard_map/while/body/eval_jaxpr/gather | solution.py:10
  161.7 4.4 %copy.10 = f32[4,8,128,256]{3,1,2,0:T(8,128)} copy(f32[4,8,128,256]{3,2,1,0:T(8,128)S(1)} %bitcast.21) | data formatting | bytes 8388608 | tf_op jit(solution)/shard_map/while
  166.1 7.4 %scatter_fusion = f32[16,32768]{1,0:T(8,128)S(1)} fusion(f32[16,32768]{1,0:T(8,128)S(1)} %get-tuple-element.117, s32[32]{0:T(128)S(1)} %get-tuple-element.104, f32[32,32768]{1,0:T(8,128)} %bitcast.22), kind=kCustom, calls=%fused_computation.1.clone.1 | custom fusion | flops 1048576 | bytes 12583040 | tf_op jit(solution)/shard_map/while/body/eval_jaxpr/scatter-add | solution.py:14
  184.0 4.4 %copy.10 = f32[4,8,128,256]{3,1,2,0:T(8,128)} copy(f32[4,8,128,256]{3,2,1,0:T(8,128)S(1)} %bitcast.21) | data formatting | bytes 8388608 | tf_op jit(solution)/shard_map/while
  188.3 7.4 %scatter_fusion = f32[16,32768]{1,0:T(8,128)S(1)} fusion(f32[16,32768]{1,0:T(8,128)S(1)} %get-tuple-element.117, s32[32]{0:T(128)S(1)} %get-tuple-element.104, f32[32,32768]{1,0:T(8,128)} %bitcast.22), kind=kCustom, calls=%fused_computation.1.clone.1 | custom fusion | flops 1048576 | bytes 12583040 | tf_op jit(solution)/shard_map/while/body/eval_jaxpr/scatter-add | solution.py:14
  206.2 4.4 %copy.10 = f32[4,8,128,256]{3,1,2,0:T(8,128)} copy(f32[4,8,128,256]{3,2,1,0:T(8,128)S(1)} %bitcast.21) | data formatting | bytes 8388608 | tf_op jit(solution)/shard_map/while
  210.6 7.4 %scatter_fusion = f32[16,32768]{1,0:T(8,128)S(1)} fusion(f32[16,32768]{1,0:T(8,128)S(1)} %get-tuple-element.117, s32[32]{0:T(128)S(1)} %get-tuple-element.104, f32[32,32768]{1,0:T(8,128)} %bitcast.22), kind=kCustom, calls=%fused_computation.1.clone.1 | custom fusion | flops 1048576 | bytes 12583040 | tf_op jit(solution)/shard_map/while/body/eval_jaxpr/scatter-add | solution.py:14
  220.3 43.1 %reduce-scatter.2.cloned.1.call-done = f32[512,256]{1,0:T(8,128)} async-done(((f32[2048,256]{1,0:T(8,128)}), f32[512,256]{1,0:T(8,128)}) %reduce-scatter.2.cloned.1.call-update) | async-done | bytes 524304 | tf_op jit(solution)/shard_map/reduce_scatter | solution.py:35
  (71 shorter events, 54.2 us)
Async XLA Ops:
  6.5 258.1 %copy-start = (bf16[512,256]{1,0:T(8,128)(2,1)S(1)}, bf16[512,256]{1,0:T(8,128)(2,1)}, u32[]{:S(2)}) copy-start(bf16[512,256]{1,0:T(8,128)(2,1)} %param.14) | copy-start | bytes 786436
  6.5 33.4 %copy-start.2 = (s32[256,2]{0,1:T(2,128)S(1)}, s32[256,2]{0,1:T(2,128)}, u32[]{:S(2)}) copy-start(s32[256,2]{0,1:T(2,128)} %param.11) | copy-start | bytes 6148
  6.5 33.2 %all-gather.2.cloned.1.call-start = ((), (), s32[]{:S(2)}) async-start(), calls=%async_computation.1 | async-start | bytes 2359296 | tf_op jit(solution)/shard_map/all_gather | solution.py:21
  7.3 256.2 %reduce-scatter.2.cloned.1.call-start = ((), (), s32[]{:S(2)}) async-start(), calls=%async_computation.2 | async-start | bytes 2621440 | tf_op jit(solution)/shard_map/reduce_scatter | solution.py:35
  219.6 0.7 copy-start.3
  219.6 45.0 %copy-start.1 = (bf16[512,256]{1,0:T(8,128)(2,1)S(1)}, bf16[512,256]{1,0:T(8,128)(2,1)}, u32[]{:S(2)}) copy-start(bf16[512,256]{1,0:T(8,128)(2,1)} %param.9) | copy-start | bytes 786436
  219.6 45.0 %copy-start.4 = (f32[256]{0:T(256)S(1)}, f32[256]{0:T(256)}, u32[]{:S(2)}) copy-start(f32[256]{0:T(256)} %param.15) | copy-start | bytes 3076
Sparse Core Ops, SparseCore 0:
  9.2 30.4 all-gather.1
  219.8 43.6 reduce-scatter.1
where the time goes:
time: 274 us; the launch traced here: 273 us
  waiting for transfers between devices  76.3 us (28%)
  local copies, waits for them, and re-layouts  72.1 us (26%)
  other arithmetic  71.5 us (26%)
  matrix products  22.5 us (8%)
  loops' own time  16.7 us (6%)
  between operations  13.5 us (5%)
    scatter-add x8, other arithmetic, block_terms(): return running.at[index_block[:, 0]].add(flattened)  59.6 us
    reduce_scatter x1, waiting for transfers between devices, local(): lax.psum_scatter(partial_value, 'col', scatter_dimension=0, tiled=True)  43.1 us
    while x8, local copies, waits for them, and re-layouts  35 us
    all_gather x1, waiting for transfers between devices, local(): gathered = lax.all_gather(features, 'row', axis=0, tiled=True)  32.4 us
    gather x8, local copies, waits for them, and re-layouts, block_terms(): picked = col_blocks[index_block[:, 1]]  28.9 us
    dot_general x8, matrix products, block_terms(): jnp.einsum('kij,kjf->kif', kept, picked, preferred_element_type=jnp.float32)  21.4 us
    another operation x1, loops' own time, local(): lax.scan(one_step, zeroed, jnp.arange(0, slot_total, BLK, dtype=jnp.int32))  16.7 us
    lt x8, other arithmetic, one_step(): live_block = offset + jnp.arange(BLK, dtype=jnp.int32) < live_count  10.6 us
  transfers between devices with their start and end apart: 2, of which 2 were waited for; matrix products, arithmetic and copies ran while one was open for 0% of the time, Pallas kernels for 0%

commit v1 on v0

--- a/solution.py
+++ b/solution.py
@@ -1,9 +1,17 @@
+import functools
+
 import jax
 import jax.numpy as jnp
 from jax import lax
+from jax.experimental import pallas as pl
+from jax.experimental.pallas import tpu as pltpu
 from jax.sharding import PartitionSpec as P
 
 BLK = 32
+LANES = 128
+CHUNKS = 16
+DENSE_LIMIT = 24 * 1024 * 1024
+MESH = pl.DeviceIdType.MESH
 
 
 def block_terms(running, col_blocks, index_block, tile_block, live_block):
@@ -14,7 +22,7 @@
     return running.at[index_block[:, 0]].add(flattened)
 
 
-def local(features, in_degree, tile_index, tile_count, adjacency_tiles, projection, out_bias):
+def local_sparse(features, in_degree, tile_index, tile_count, adjacency_tiles, projection, out_bias):
     feat_width = features.shape[1]
     tile_size = adjacency_tiles.shape[1]
     slot_total = adjacency_tiles.shape[0]
@@ -39,7 +47,268 @@
     return jnp.maximum(mixed, 0.0).astype(jnp.bfloat16)
 
 
+def densify_kernel(row_blocks, count_ref, place_ref, tiles_ref, dense_ref, stage, sems):
+    slots, tile = stage.shape[0], stage.shape[1]
+    per = slots // CHUNKS
+
+    def load(i):
+        part = pl.ds(i * per, per)
+        return pltpu.make_async_copy(tiles_ref.at[part], stage.at[part], sems.at[i])
+
+    for i in range(CHUNKS):
+        load(i).start()
+
+    @pl.loop(0, dense_ref.shape[0])
+    def _(j):
+        dense_ref[j] = jnp.zeros(dense_ref.shape[1:], dense_ref.dtype)
+
+    count = count_ref[0]
+    for i in range(CHUNKS):
+        load(i).wait()
+
+        @pl.loop(i * per, jnp.minimum((i + 1) * per, jnp.maximum(count, i * per)))
+        def _(slot):
+            place = place_ref[slot]
+            col = place // row_blocks
+            row = pl.multiple_of((place - col * row_blocks) * tile, tile)
+            dense_ref[col, pl.ds(row, tile), :] += stage[slot]
+
+
+def fused_kernel(n_row, n_col, feat_ref, dense_ref, degree_ref, proj_ref, bias_ref, out_ref,
+                 gathered, acc, hidden, degree_col, send_r, recv_r, send_l, recv_l,
+                 ag_send, ag_recv, sr_sem, rr_sem, sl_sem, rl_sem):
+    seg, width = feat_ref.shape
+    halves = width // LANES
+    blocks = seg // LANES
+    chips = n_row // 2
+    r = lax.axis_index("row")
+    c = lax.axis_index("col")
+    sibling = r ^ 1
+
+    barrier = pltpu.get_barrier_semaphore()
+
+    def greet(row, col):
+        pl.semaphore_signal(barrier, inc=1, device_id=(row, col), device_id_type=MESH)
+
+    greet(sibling, c)
+    for m in range(1, chips):
+        greet(r ^ (2 * m), c)
+
+    @pl.when(c > 0)
+    def _():
+        greet(r, c - 1)
+
+    @pl.when(c < n_col - 1)
+    def _():
+        greet(r, c + 1)
+
+    pl.semaphore_wait(
+        barrier, chips + jnp.where(c > 0, 1, 0) + jnp.where(c < n_col - 1, 1, 0))
+
+    def lanes(h):
+        return pl.ds(h * LANES, LANES)
+
+    def gather_copy(h, j):
+        if j == 0:
+            src, owner, target = feat_ref.at[:, lanes(h)], r, sibling
+        elif j < chips:
+            src, owner, target = feat_ref.at[:, lanes(h)], r, r ^ (2 * j)
+        else:
+            owner = r ^ (2 * (j - chips + 1))
+            src, target = gathered.at[owner, :, lanes(h)], sibling
+        return pltpu.make_async_remote_copy(
+            src_ref=src, dst_ref=gathered.at[owner, :, lanes(h)],
+            send_sem=ag_send.at[h, j], recv_sem=ag_recv.at[h, j],
+            device_id=(target, c), device_id_type=MESH)
+
+    def source(j):
+        if j == 0:
+            return sibling
+        if j < chips:
+            return r ^ (2 * j)
+        return sibling ^ (2 * (j - chips + 1))
+
+    total = 2 * chips - 1
+    for h in range(halves):
+        for j in range(1, chips):
+            gather_copy(h, j).start()
+        gather_copy(h, 0).start()
+
+    def multiply(h, owner, block, first):
+        @pl.loop(0, n_col)
+        def _(d):
+            rows = pl.ds(pl.multiple_of(d * seg, seg), seg)
+            left = jnp.concatenate(
+                [dense_ref[owner * blocks + k, rows, :] for k in range(blocks)], axis=1)
+            product = jnp.dot(left, block, preferred_element_type=jnp.float32)
+            if first:
+                acc[h, rows, :] = product
+            else:
+                acc[h, rows, :] += product
+
+    def own_block(h):
+        multiply(h, r, feat_ref[:, lanes(h)], True)
+
+    def other_block(h, j):
+        gather_copy(h, j).wait_recv()
+        if 0 < j < chips:
+            gather_copy(h, j + chips - 1).start()
+        owner = source(j)
+        multiply(h, owner, gathered[owner, :, lanes(h)], False)
+
+    def right_copy(h, d):
+        return pltpu.make_async_remote_copy(
+            src_ref=send_r.at[h, d], dst_ref=recv_r.at[h, d],
+            send_sem=sr_sem.at[h, d], recv_sem=rr_sem.at[h, d],
+            device_id=(r, c + 1), device_id_type=MESH)
+
+    def left_copy(h, d):
+        return pltpu.make_async_remote_copy(
+            src_ref=send_l.at[h, d], dst_ref=recv_l.at[h, d],
+            send_sem=sl_sem.at[h, d], recv_sem=rl_sem.at[h, d],
+            device_id=(r, c - 1), device_id_type=MESH)
+
+    def term(h, d):
+        return acc[h, d * seg:(d + 1) * seg, :]
+
+    def begin(h):
+        @pl.when(c == 0)
+        def _():
+            for d in range(n_col - 1, 0, -1):
+                send_r[h, d] = term(h, d).astype(send_r.dtype)
+                right_copy(h, d).start()
+
+        @pl.when(c == n_col - 1)
+        def _():
+            for d in range(n_col - 1):
+                send_l[h, d] = term(h, d).astype(send_l.dtype)
+                left_copy(h, d).start()
+
+    def relay(h, t):
+        d = n_col - 1 - t
+
+        @pl.when((c > 0) & (c < d))
+        def _():
+            right_copy(h, d).wait_recv()
+            send_r[h, d] = (term(h, d) + recv_r[h, d].astype(jnp.float32)).astype(send_r.dtype)
+            right_copy(h, d).start()
+
+        @pl.when((c < n_col - 1) & (c > t))
+        def _():
+            left_copy(h, t).wait_recv()
+            send_l[h, t] = (term(h, t) + recv_l[h, t].astype(jnp.float32)).astype(send_l.dtype)
+            left_copy(h, t).start()
+
+    def finish(h):
+        own = pl.ds(pl.multiple_of(c * seg, seg), seg)
+
+        @pl.when(c > 0)
+        def _():
+            right_copy(h, c).wait_recv()
+            acc[h, own, :] += recv_r[h, c].astype(jnp.float32)
+
+        @pl.when(c < n_col - 1)
+        def _():
+            left_copy(h, c).wait_recv()
+            acc[h, own, :] += recv_l[h, c].astype(jnp.float32)
+
+        mean = (acc[h, own, :] / degree_col[...]).astype(jnp.bfloat16)
+        hidden[...] += jnp.dot(
+            mean, proj_ref[width + h * LANES:width + (h + 1) * LANES, :],
+            preferred_element_type=jnp.float32)
+
+    for h in range(halves):
+        own_block(h)
+        if h == 0:
+            hidden[...] = jnp.dot(
+                feat_ref[...], proj_ref[:width, :],
+                preferred_element_type=jnp.float32) + bias_ref[...]
+            for b in range(blocks):
+                one = degree_ref[b:b + 1, :].astype(jnp.float32)
+                degree_col[b * LANES:(b + 1) * LANES, :] = jnp.transpose(
+                    jnp.broadcast_to(one, (LANES, LANES)))
+        for j in range(total):
+            other_block(h, j)
+            if h > 0 and j >= 2 and j % 2 == 0 and (j - 2) // 2 < n_col - 2:
+                relay(h - 1, (j - 2) // 2)
+        begin(h)
+        if h > 0:
+            finish(h - 1)
+    for t in range(n_col - 2):
+        relay(halves - 1, t)
+    finish(halves - 1)
+    out_ref[...] = jnp.maximum(hidden[...], 0.0).astype(out_ref.dtype)
+
+    for h in range(halves):
+        for j in range(total):
+            gather_copy(h, j).wait_send()
+        for d in range(n_col):
+            if d > 0:
+                @pl.when(c < d)
+                def _():
+                    right_copy(h, d).wait_send()
+            if d < n_col - 1:
+                @pl.when(c > d)
+                def _():
+                    left_copy(h, d).wait_send()
+
+
+def local_dense(n_row, n_col, features, in_degree, tile_index, tile_count, adjacency_tiles, projection, out_bias):
+    seg, width = features.shape
+    slots, tile, _ = adjacency_tiles.shape
+    row_blocks = seg * n_col // tile
+    col_blocks = seg * n_row // tile
+    halves = width // LANES
+    vmem = pl.BlockSpec(memory_space=pltpu.VMEM)
+    smem = pl.BlockSpec(memory_space=pltpu.SMEM)
+    place = tile_index[:, 0] + tile_index[:, 1] * row_blocks
+    dense = pl.pallas_call(
+        functools.partial(densify_kernel, row_blocks),
+        out_shape=pltpu.VMEM((col_blocks, row_blocks * tile, tile), jnp.bfloat16),
+        in_specs=[smem, smem, pl.BlockSpec(memory_space=pl.ANY)],
+        out_specs=vmem,
+        scratch_shapes=[
+            pltpu.VMEM((slots, tile, tile), jnp.bfloat16),
+            pltpu.SemaphoreType.DMA((CHUNKS,)),
+        ],
+        compiler_params=pltpu.CompilerParams(vmem_limit_bytes=42 * 1024 * 1024),
+    )(tile_count, place, adjacency_tiles)
+    carry = pltpu.VMEM((halves, n_col, seg, LANES), jnp.bfloat16)
+    carry_sem = pltpu.SemaphoreType.DMA((halves, n_col))
+    gather_sem = pltpu.SemaphoreType.DMA((halves, n_row))
+    return pl.pallas_call(
+        functools.partial(fused_kernel, n_row, n_col),
+        out_shape=jax.ShapeDtypeStruct((seg, projection.shape[1]), jnp.bfloat16),
+        in_specs=[vmem] * 5,
+        out_specs=vmem,
+        scratch_shapes=[
+            pltpu.VMEM((n_row, seg, width), jnp.bfloat16),
+            pltpu.VMEM((halves, n_col * seg, LANES), jnp.float32),
+            pltpu.VMEM((seg, projection.shape[1]), jnp.float32),
+            pltpu.VMEM((seg, LANES), jnp.float32),
+            carry, carry, carry, carry,
+            gather_sem, gather_sem,
+            carry_sem, carry_sem, carry_sem, carry_sem,
+        ],
+        compiler_params=pltpu.CompilerParams(
+            collective_id=0, has_side_effects=True, vmem_limit_bytes=24 * 1024 * 1024),
+    )(features, dense, in_degree.reshape(seg // LANES, LANES), projection, out_bias[None, :])
+
+
 def solution(mesh):
+    n_row, n_col = mesh.shape["row"], mesh.shape["col"]
+
+    def local(features, in_degree, tile_index, tile_count, adjacency_tiles, projection, out_bias):
+        seg, width = features.shape
+        slots, tile, _ = adjacency_tiles.shape
+        dense_bytes = 2 * seg * n_row * seg * n_col
+        fits = (
+            dense_bytes <= DENSE_LIMIT and slots <= 256 and slots % CHUNKS == 0
+            and tile == LANES and seg % LANES == 0 and width % LANES == 0
+            and n_row >= 4 and n_row & (n_row - 1) == 0 and n_col >= 2)
+        args = (features, in_degree, tile_index, tile_count, adjacency_tiles, projection, out_bias)
+        return local_dense(n_row, n_col, *args) if fits else local_sparse(*args)
+
     return jax.shard_map(
         local,
         mesh=mesh,

time: 274 us -> 60.7 us (0.22)
  waiting for transfers between devices: 76.3 us -> 0 us
  local copies, waits for them, and re-layouts: 72.1 us -> 0.72 us
  other arithmetic: 71.5 us -> 1.32 us
  Pallas kernels: 0 us -> 57.7 us
  matrix products: 22.5 us -> 0 us
  loops' own time: 16.7 us -> 0 us
  between operations: 13.5 us -> 0.76 us
    scatter-add x8 -> x0, other arithmetic: 59.6 us -> none  [block_terms(): return running.at[index_block[:, 0]].add(flattened)]
    pallas_call x0 -> x2, Pallas kernels: none -> 57.7 us  [the longest x1 52.1 us: local_dense(): pl.pallas_call(functools.partial(fused_kernel, n_row, n_col), out_shape=j...]
    reduce_scatter x1 -> x0, waiting for transfers between devices: 43.1 us -> none  [local(): lax.psum_scatter(partial_value, 'col', scatter_dimension=0, tiled=True)]
    while x8 -> x0, local copies, waits for them, and re-layouts: 35 us -> none
    all_gather x1 -> x0, waiting for transfers between devices: 32.4 us -> none  [local(): gathered = lax.all_gather(features, 'row', axis=0, tiled=True)]
    gather x8 -> x0, local copies, waits for them, and re-layouts: 28.9 us -> none  [block_terms(): picked = col_blocks[index_block[:, 1]]]
    dot_general x9 -> x0, matrix products: 22.5 us -> none  [the longest x8 21.4 us: block_terms(): jnp.einsum('kij,kjf->kif', kept, picked, preferred_element_type=jnp.float32)]
    another operation x1 -> x0, loops' own time: 16.7 us -> none  [local(): lax.scan(one_step, zeroed, jnp.arange(0, slot_total, BLK, dtype=jnp.int32))]
  transfers between devices with their start and end apart: 2 -> 0, of which waited for: 2 -> 0; matrix products, arithmetic and copies ran while one was open for 0% -> 0% of each run, Pallas kernels for 0% -> 0%
where the time goes in v1:
time: 60.7 us; the launch traced here: 60.5 us
  Pallas kernels  57.7 us (95%)
  other arithmetic  1.32 us (2%)
  between operations  0.76 us (1%)
  local copies, waits for them, and re-layouts  0.72 us (1%)
    pallas_call x1, Pallas kernels, local_dense(): pl.pallas_call(functools.partial(fused_kernel, n_row, n_col), out_shape=j...  52.1 us
    pallas_call x1, Pallas kernels, local_dense(): pl.pallas_call(functools.partial(densify_kernel, row_blocks), out_shape=p...  5.52 us
    add x1, other arithmetic, local_dense(): place = tile_index[:, 0] + tile_index[:, 1] * row_blocks  1.32 us

profile of v1, /device:TPU:0, one launch (start us, length us, event | category | flops | bytes accessed | tf_op | source)
XLA Modules:
  0.0 60.5 jit_solution(16750348563340150177)
XLA Ops:
  0.0 0.0 copy-start.3
  0.0 0.0 copy-start.1
  0.0 0.0 copy-start.2
  0.0 0.0 copy-start
  0.7 1.3 %multiply_add_fusion = s32[256,1]{0,1:T(1,128)} fusion(s32[256,2]{0,1:T(2,128)} %param.9), kind=kLoop, calls=%fused_computation | loop fusion | flops 512 | bytes 3072 | tf_op jit(solution)/shard_map/add | solution.py:264
  2.0 5.5 %shard_map.73.dense_ref = bf16[32,2048,128]{2,1,0:T(8,128)(2,1)S(1)} custom-call(s32[1]{0:T(128)S(6)} %copy.9.count_ref, s32[256]{0:T(256)} %bitcast.5, bf16[256,128,128]{2,1,0:T(8,128)(2,1)} %tiles_ref.1), custom_call_target="tpu_custom_call" | custom-call | tf_op jit(solution)/shard_map/pallas_call | solution.py:265
  7.6 0.0 copy-done.3
  7.6 0.0 copy-done.1
  7.6 0.0 copy-done.2
  7.6 0.0 copy-done
  7.6 52.1 %shard_map.74 = bf16[512,256]{1,0:T(8,128)(2,1)S(1)} custom-call(bf16[512,256]{1,0:T(8,128)(2,1)S(1)} %copy-done, bf16[32,2048,128]{2,1,0:T(8,128)(2,1)S(1)} %shard_map.73.dense_ref, s32[4,128]{1,0:T(4,128)S(1)} %bitcast.3, bf16[512,256]{1,0:T(8,128)(2,1)S(1)} %copy-done.1, f32[1,256]{1,0:T(1,128)S(1)} %bitcast.4), custom_call_target="tpu_custom_call" | custom-call | tf_op jit(solution)/shard_map/pallas_call | solution.py:279
  59.8 0.7 %copy.10 = bf16[512,256]{1,0:T(8,128)(2,1)} copy(bf16[512,256]{1,0:T(8,128)(2,1)S(1)} %shard_map.74) | data formatting | bytes 524288
Async XLA Ops:
  0.0 7.6 %copy-start.3 = (f32[256]{0:T(256)S(1)}, f32[256]{0:T(256)}, u32[]{:S(2)}) copy-start(f32[256]{0:T(256)} %param.13) | copy-start | bytes 3076
  0.0 7.6 %copy-start.1 = (bf16[512,256]{1,0:T(8,128)(2,1)S(1)}, bf16[512,256]{1,0:T(8,128)(2,1)}, u32[]{:S(2)}) copy-start(bf16[512,256]{1,0:T(8,128)(2,1)} %proj_ref.1) | copy-start | bytes 786436
  0.0 7.6 %copy-start.2 = (s32[512]{0:T(512)S(1)}, s32[512]{0:T(512)}, u32[]{:S(2)}) copy-start(s32[512]{0:T(512)} %param.8) | copy-start | bytes 6148
  0.0 7.6 %copy-start = (bf16[512,256]{1,0:T(8,128)(2,1)S(1)}, bf16[512,256]{1,0:T(8,128)(2,1)}, u32[]{:S(2)}) copy-start(bf16[512,256]{1,0:T(8,128)(2,1)} %feat_ref.1) | copy-start | bytes 786436

commit v2 on v1

--- a/solution.py
+++ b/solution.py
@@ -75,8 +75,8 @@
 
 
 def fused_kernel(n_row, n_col, feat_ref, dense_ref, degree_ref, proj_ref, bias_ref, out_ref,
-                 gathered, acc, hidden, degree_col, send_r, recv_r, send_l, recv_l,
-                 ag_send, ag_recv, sr_sem, rr_sem, sl_sem, rl_sem):
+                 gathered, acc, hidden, degree_col, send, relayed, landed,
+                 ag_send, ag_recv, send_sem, relay_sem, land_sem):
     seg, width = feat_ref.shape
     halves = width // LANES
     blocks = seg // LANES
@@ -94,16 +94,17 @@
     for m in range(1, chips):
         greet(r ^ (2 * m), c)
 
-    @pl.when(c > 0)
-    def _():
-        greet(r, c - 1)
-
-    @pl.when(c < n_col - 1)
-    def _():
-        greet(r, c + 1)
-
-    pl.semaphore_wait(
-        barrier, chips + jnp.where(c > 0, 1, 0) + jnp.where(c < n_col - 1, 1, 0))
+    peers = chips
+    for hop in range(1, n_col):
+        for step in (-hop, hop):
+            inside = (c + step >= 0) & (c + step < n_col)
+            peers = peers + jnp.where(inside, 1, 0)
+
+            @pl.when(inside)
+            def _():
+                greet(r, c + step)
+
+    pl.semaphore_wait(barrier, peers)
 
     def lanes(h):
         return pl.ds(h * LANES, LANES)
@@ -129,10 +130,13 @@
         return sibling ^ (2 * (j - chips + 1))
 
     total = 2 * chips - 1
-    for h in range(halves):
+
+    def gather_start(h):
         for j in range(1, chips):
             gather_copy(h, j).start()
         gather_copy(h, 0).start()
+
+    gather_start(0)
 
     def multiply(h, owner, block, first):
         @pl.loop(0, n_col)
@@ -156,61 +160,83 @@
         owner = source(j)
         multiply(h, owner, gathered[owner, :, lanes(h)], False)
 
-    def right_copy(h, d):
-        return pltpu.make_async_remote_copy(
-            src_ref=send_r.at[h, d], dst_ref=recv_r.at[h, d],
-            send_sem=sr_sem.at[h, d], recv_sem=rr_sem.at[h, d],
-            device_id=(r, c + 1), device_id_type=MESH)
-
-    def left_copy(h, d):
-        return pltpu.make_async_remote_copy(
-            src_ref=send_l.at[h, d], dst_ref=recv_l.at[h, d],
-            send_sem=sl_sem.at[h, d], recv_sem=rl_sem.at[h, d],
-            device_id=(r, c - 1), device_id_type=MESH)
-
     def term(h, d):
         return acc[h, d * seg:(d + 1) * seg, :]
 
-    def begin(h):
-        @pl.when(c == 0)
-        def _():
-            for d in range(n_col - 1, 0, -1):
-                send_r[h, d] = term(h, d).astype(send_r.dtype)
-                right_copy(h, d).start()
-
-        @pl.when(c == n_col - 1)
-        def _():
-            for d in range(n_col - 1):
-                send_l[h, d] = term(h, d).astype(send_l.dtype)
-                left_copy(h, d).start()
-
-    def relay(h, t):
-        d = n_col - 1 - t
-
-        @pl.when((c > 0) & (c < d))
-        def _():
-            right_copy(h, d).wait_recv()
-            send_r[h, d] = (term(h, d) + recv_r[h, d].astype(jnp.float32)).astype(send_r.dtype)
-            right_copy(h, d).start()
-
-        @pl.when((c < n_col - 1) & (c > t))
-        def _():
-            left_copy(h, t).wait_recv()
-            send_l[h, t] = (term(h, t) + recv_l[h, t].astype(jnp.float32)).astype(send_l.dtype)
-            left_copy(h, t).start()
+    def relay_copy(h, d, way):
+        return pltpu.make_async_remote_copy(
+            src_ref=send.at[h, d], dst_ref=relayed.at[h],
+            send_sem=send_sem.at[h, d], recv_sem=relay_sem.at[h],
+            device_id=(r, c + way), device_id_type=MESH)
+
+    def land_copy(h, d, slot):
+        return pltpu.make_async_remote_copy(
+            src_ref=send.at[h, d], dst_ref=landed.at[h, slot],
+            send_sem=send_sem.at[h, d], recv_sem=land_sem.at[h, slot],
+            device_id=(r, d), device_id_type=MESH)
+
+    def routes():
+        for d in range(n_col - 1, -1, -1):
+            for c_from in range(n_col):
+                if c_from != d:
+                    yield d, c_from, abs(d - c_from), 1 if d > c_from else -1
+
+    def slot_of(hops, way):
+        return hops - 1 + (0 if way > 0 else 2)
+
+    def adds_relay(d, c_from, hops, way):
+        return hops == 2 and 0 <= c_from - way < n_col
+
+    def relays(c_from):
+        return n_col == 4 and c_from in (0, n_col - 1)
+
+    def send_direct(h, d, hops, way):
+        send[h, d] = term(h, d).astype(send.dtype)
+        land_copy(h, d, slot_of(hops, way)).start()
+
+    def first_sends(h):
+        for d, c_from, hops, way in routes():
+            if hops == 3:
+                @pl.when(c == c_from)
+                def _():
+                    send[h, d] = term(h, d).astype(send.dtype)
+                    relay_copy(h, d, way).start()
+            elif not relays(c_from) and not adds_relay(d, c_from, hops, way):
+                @pl.when(c == c_from)
+                def _():
+                    send_direct(h, d, hops, way)
+
+    def later_sends(h):
+        for c_from in range(n_col):
+            if relays(c_from):
+                @pl.when(c == c_from)
+                def _():
+                    far = n_col - 1 - c_from
+                    way = 1 if far > c_from else -1
+                    relay_copy(h, far, way).wait_send()
+                    for hops in (2, 1):
+                        send_direct(h, c_from + way * hops, hops, way)
+
+    def relay_sends(h):
+        for d, c_from, hops, way in routes():
+            if adds_relay(d, c_from, hops, way):
+                @pl.when(c == c_from)
+                def _():
+                    relay_copy(h, d, way).wait_recv()
+                    send[h, d] = (term(h, d) + relayed[h].astype(jnp.float32)).astype(send.dtype)
+                    land_copy(h, d, slot_of(hops, way)).start()
 
     def finish(h):
         own = pl.ds(pl.multiple_of(c * seg, seg), seg)
-
-        @pl.when(c > 0)
-        def _():
-            right_copy(h, c).wait_recv()
-            acc[h, own, :] += recv_r[h, c].astype(jnp.float32)
-
-        @pl.when(c < n_col - 1)
-        def _():
-            left_copy(h, c).wait_recv()
-            acc[h, own, :] += recv_l[h, c].astype(jnp.float32)
+        for hops in (1, 2):
+            for way in (1, -1):
+                origin = c - way * hops
+
+                @pl.when((origin >= 0) & (origin < n_col))
+                def _():
+                    slot = slot_of(hops, way)
+                    land_copy(h, 0, slot).wait_recv()
+                    acc[h, own, :] += landed[h, slot].astype(jnp.float32)
 
         mean = (acc[h, own, :] / degree_col[...]).astype(jnp.bfloat16)
         hidden[...] += jnp.dot(
@@ -228,29 +254,28 @@
                 degree_col[b * LANES:(b + 1) * LANES, :] = jnp.transpose(
                     jnp.broadcast_to(one, (LANES, LANES)))
         for j in range(total):
+            if h > 0 and j == 1:
+                later_sends(h - 1)
+                relay_sends(h - 1)
             other_block(h, j)
-            if h > 0 and j >= 2 and j % 2 == 0 and (j - 2) // 2 < n_col - 2:
-                relay(h - 1, (j - 2) // 2)
-        begin(h)
+            if j == chips - 1 and h + 1 < halves:
+                gather_start(h + 1)
+        first_sends(h)
         if h > 0:
             finish(h - 1)
-    for t in range(n_col - 2):
-        relay(halves - 1, t)
+    later_sends(halves - 1)
+    relay_sends(halves - 1)
     finish(halves - 1)
     out_ref[...] = jnp.maximum(hidden[...], 0.0).astype(out_ref.dtype)
 
     for h in range(halves):
         for j in range(total):
             gather_copy(h, j).wait_send()
-        for d in range(n_col):
-            if d > 0:
-                @pl.when(c < d)
-                def _():
-                    right_copy(h, d).wait_send()
-            if d < n_col - 1:
-                @pl.when(c > d)
-                def _():
-                    left_copy(h, d).wait_send()
+        for d, c_from, hops, way in routes():
+            if hops < 3:
+                @pl.when(c == c_from)
+                def _():
+                    land_copy(h, d, slot_of(hops, way)).wait_send()
 
 
 def local_dense(n_row, n_col, features, in_degree, tile_index, tile_count, adjacency_tiles, projection, out_bias):
@@ -273,8 +298,7 @@
         ],
         compiler_params=pltpu.CompilerParams(vmem_limit_bytes=42 * 1024 * 1024),
     )(tile_count, place, adjacency_tiles)
-    carry = pltpu.VMEM((halves, n_col, seg, LANES), jnp.bfloat16)
-    carry_sem = pltpu.SemaphoreType.DMA((halves, n_col))
+    carry_sem = pltpu.SemaphoreType.DMA((halves, 4))
     gather_sem = pltpu.SemaphoreType.DMA((halves, n_row))
     return pl.pallas_call(
         functools.partial(fused_kernel, n_row, n_col),
@@ -286,9 +310,11 @@
             pltpu.VMEM((halves, n_col * seg, LANES), jnp.float32),
             pltpu.VMEM((seg, projection.shape[1]), jnp.float32),
             pltpu.VMEM((seg, LANES), jnp.float32),
-            carry, carry, carry, carry,
+            pltpu.VMEM((halves, n_col, seg, LANES), jnp.bfloat16),
+            pltpu.VMEM((halves, seg, LANES), jnp.bfloat16),
+            pltpu.VMEM((halves, 4, seg, LANES), jnp.bfloat16),
             gather_sem, gather_sem,
-            carry_sem, carry_sem, carry_sem, carry_sem,
+            carry_sem, pltpu.SemaphoreType.DMA((halves,)), carry_sem,
         ],
         compiler_params=pltpu.CompilerParams(
             collective_id=0, has_side_effects=True, vmem_limit_bytes=24 * 1024 * 1024),
@@ -305,7 +331,7 @@
         fits = (
             dense_bytes <= DENSE_LIMIT and slots <= 256 and slots % CHUNKS == 0
             and tile == LANES and seg % LANES == 0 and width % LANES == 0
-            and n_row >= 4 and n_row & (n_row - 1) == 0 and n_col >= 2)
+            and n_row >= 4 and n_row & (n_row - 1) == 0 and 2 <= n_col <= 4)
         args = (features, in_degree, tile_index, tile_count, adjacency_tiles, projection, out_bias)
         return local_dense(n_row, n_col, *args) if fits else local_sparse(*args)
 

time: 60.7 us -> 50.7 us (0.84)
  Pallas kernels: 57.7 us -> 48 us
    pallas_call x1, Pallas kernels: 52.1 us -> 43.4 us  [local_dense(): pl.pallas_call(functools.partial(fused_kernel, n_row, n_col), out_shape=j...]
    pallas_call x1, Pallas kernels: 5.52 us -> 4.65 us  [local_dense(): pl.pallas_call(functools.partial(densify_kernel, row_blocks), out_shape=p...]
where the time goes in v2:
time: 50.7 us; the launch traced here: 50.8 us
  Pallas kernels  48 us (95%)
  other arithmetic  1.32 us (3%)
  between operations  0.76 us (1%)
  local copies, waits for them, and re-layouts  0.72 us (1%)
    pallas_call x1, Pallas kernels, local_dense(): pl.pallas_call(functools.partial(fused_kernel, n_row, n_col), out_shape=j...  43.4 us
    pallas_call x1, Pallas kernels, local_dense(): pl.pallas_call(functools.partial(densify_kernel, row_blocks), out_shape=p...  4.65 us
    add x1, other arithmetic, local_dense(): place = tile_index[:, 0] + tile_index[:, 1] * row_blocks  1.32 us

profile of v2, /device:TPU:0, one launch (start us, length us, event | category | flops | bytes accessed | tf_op | source)
XLA Modules:
  0.0 50.8 jit_solution(11445685629109093623)
XLA Ops:
  0.0 0.0 copy-start.3
  0.0 0.0 copy-start.1
  0.0 0.0 copy-start.2
  0.0 0.0 copy-start
  0.7 1.3 %multiply_add_fusion = s32[256,1]{0,1:T(1,128)} fusion(s32[256,2]{0,1:T(2,128)} %param.9), kind=kLoop, calls=%fused_computation | loop fusion | flops 512 | bytes 3072 | tf_op jit(solution)/shard_map/add | solution.py:289
  2.0 4.6 %shard_map.73.dense_ref = bf16[32,2048,128]{2,1,0:T(8,128)(2,1)S(1)} custom-call(s32[1]{0:T(128)S(6)} %copy.9.count_ref, s32[256]{0:T(256)} %bitcast.5, bf16[256,128,128]{2,1,0:T(8,128)(2,1)} %tiles_ref.1), custom_call_target="tpu_custom_call" | custom-call | tf_op jit(solution)/shard_map/pallas_call | solution.py:290
  6.7 0.0 copy-done.3
  6.7 0.0 copy-done.1
  6.7 0.0 copy-done.2
  6.7 0.0 copy-done
  6.7 43.4 %shard_map.74 = bf16[512,256]{1,0:T(8,128)(2,1)S(1)} custom-call(bf16[512,256]{1,0:T(8,128)(2,1)S(1)} %copy-done, bf16[32,2048,128]{2,1,0:T(8,128)(2,1)S(1)} %shard_map.73.dense_ref, s32[4,128]{1,0:T(4,128)S(1)} %bitcast.3, bf16[512,256]{1,0:T(8,128)(2,1)S(1)} %copy-done.1, f32[1,256]{1,0:T(1,128)S(1)} %bitcast.4), custom_call_target="tpu_custom_call" | custom-call | tf_op jit(solution)/shard_map/pallas_call | solution.py:303
  50.1 0.7 %copy.10 = bf16[512,256]{1,0:T(8,128)(2,1)} copy(bf16[512,256]{1,0:T(8,128)(2,1)S(1)} %shard_map.74) | data formatting | bytes 524288
Async XLA Ops:
  0.0 6.7 %copy-start.3 = (f32[256]{0:T(256)S(1)}, f32[256]{0:T(256)}, u32[]{:S(2)}) copy-start(f32[256]{0:T(256)} %param.13) | copy-start | bytes 3076
  0.0 6.7 %copy-start.1 = (bf16[512,256]{1,0:T(8,128)(2,1)S(1)}, bf16[512,256]{1,0:T(8,128)(2,1)}, u32[]{:S(2)}) copy-start(bf16[512,256]{1,0:T(8,128)(2,1)} %proj_ref.1) | copy-start | bytes 786436
  0.0 6.7 %copy-start.2 = (s32[512]{0:T(512)S(1)}, s32[512]{0:T(512)}, u32[]{:S(2)}) copy-start(s32[512]{0:T(512)} %param.8) | copy-start | bytes 6148
  0.0 6.7 %copy-start = (bf16[512,256]{1,0:T(8,128)(2,1)S(1)}, bf16[512,256]{1,0:T(8,128)(2,1)}, u32[]{:S(2)}) copy-start(bf16[512,256]{1,0:T(8,128)(2,1)} %feat_ref.1) | copy-start | bytes 786436

commit v3 on v2

--- a/solution.py
+++ b/solution.py
@@ -47,7 +47,7 @@
     return jnp.maximum(mixed, 0.0).astype(jnp.bfloat16)
 
 
-def densify_kernel(row_blocks, count_ref, place_ref, tiles_ref, dense_ref, stage, sems):
+def densify_kernel(count_ref, place_ref, tiles_ref, dense_ref, stage, sems):
     slots, tile = stage.shape[0], stage.shape[1]
     per = slots // CHUNKS
 
@@ -68,9 +68,8 @@
 
         @pl.loop(i * per, jnp.minimum((i + 1) * per, jnp.maximum(count, i * per)))
         def _(slot):
-            place = place_ref[slot]
-            col = place // row_blocks
-            row = pl.multiple_of((place - col * row_blocks) * tile, tile)
+            col = place_ref[1, slot]
+            row = pl.multiple_of(place_ref[0, slot] * tile, tile)
             dense_ref[col, pl.ds(row, tile), :] += stage[slot]
 
 
@@ -286,9 +285,8 @@
     halves = width // LANES
     vmem = pl.BlockSpec(memory_space=pltpu.VMEM)
     smem = pl.BlockSpec(memory_space=pltpu.SMEM)
-    place = tile_index[:, 0] + tile_index[:, 1] * row_blocks
     dense = pl.pallas_call(
-        functools.partial(densify_kernel, row_blocks),
+        densify_kernel,
         out_shape=pltpu.VMEM((col_blocks, row_blocks * tile, tile), jnp.bfloat16),
         in_specs=[smem, smem, pl.BlockSpec(memory_space=pl.ANY)],
         out_specs=vmem,
@@ -297,7 +295,7 @@
             pltpu.SemaphoreType.DMA((CHUNKS,)),
         ],
         compiler_params=pltpu.CompilerParams(vmem_limit_bytes=42 * 1024 * 1024),
-    )(tile_count, place, adjacency_tiles)
+    )(tile_count, tile_index.T, adjacency_tiles)
     carry_sem = pltpu.SemaphoreType.DMA((halves, 4))
     gather_sem = pltpu.SemaphoreType.DMA((halves, n_row))
     return pl.pallas_call(

time: 50.7 us -> 48.1 us (0.949)
  Pallas kernels: 48 us -> 46.4 us
  other arithmetic: 1.32 us -> 0 us
    add x1 -> x0, other arithmetic: 1.32 us -> none  [local_dense(): place = tile_index[:, 0] + tile_index[:, 1] * row_blocks]
    pallas_call x1, Pallas kernels: 43.4 us -> 42.2 us  [local_dense(): pl.pallas_call(functools.partial(fused_kernel, n_row, n_col), out_shape=j...]
where the time goes in v3:
time: 48.1 us; the launch traced here: 47.9 us
  Pallas kernels  46.4 us (96%)
  between operations  0.76 us (2%)
  local copies, waits for them, and re-layouts  0.72 us (1%)
    pallas_call x1, Pallas kernels, local_dense(): pl.pallas_call(functools.partial(fused_kernel, n_row, n_col), out_shape=j...  42.2 us
    pallas_call x1, Pallas kernels, local_dense(): pl.pallas_call(densify_kernel, out_shape=pltpu.VMEM((col_blocks, row_bloc...  4.2 us

profile of v3, /device:TPU:0, one launch (start us, length us, event | category | flops | bytes accessed | tf_op | source)
XLA Modules:
  0.0 47.9 jit_solution(14950645598390619264)
XLA Ops:
  0.0 0.0 copy-start.3
  0.0 0.0 copy-start.1
  0.0 0.0 copy-start.2
  0.0 0.0 copy-start
  0.7 4.2 %shard_map.73.dense_ref = bf16[32,2048,128]{2,1,0:T(8,128)(2,1)S(1)} custom-call(s32[1]{0:T(128)S(6)} %copy.9.count_ref, s32[2,256]{1,0:T(2,128)} %bitcast.5, bf16[256,128,128]{2,1,0:T(8,128)(2,1)} %tiles_ref.1), custom_call_target="tpu_custom_call" | custom-call | tf_op jit(solution)/shard_map/pallas_call | solution.py:288
  4.9 0.0 copy-done.3
  4.9 0.0 copy-done.1
  5.0 0.0 copy-done.2
  5.0 0.0 copy-done
  5.0 42.2 %shard_map.74 = bf16[512,256]{1,0:T(8,128)(2,1)S(1)} custom-call(bf16[512,256]{1,0:T(8,128)(2,1)S(1)} %copy-done, bf16[32,2048,128]{2,1,0:T(8,128)(2,1)S(1)} %shard_map.73.dense_ref, s32[4,128]{1,0:T(4,128)S(1)} %bitcast.3, bf16[512,256]{1,0:T(8,128)(2,1)S(1)} %copy-done.1, f32[1,256]{1,0:T(1,128)S(1)} %bitcast.4), custom_call_target="tpu_custom_call" | custom-call | tf_op jit(solution)/shard_map/pallas_call | solution.py:301
  47.2 0.7 %copy.10 = bf16[512,256]{1,0:T(8,128)(2,1)} copy(bf16[512,256]{1,0:T(8,128)(2,1)S(1)} %shard_map.74) | data formatting | bytes 524288
Async XLA Ops:
  0.0 4.9 %copy-start.3 = (f32[256]{0:T(256)S(1)}, f32[256]{0:T(256)}, u32[]{:S(2)}) copy-start(f32[256]{0:T(256)} %param.13) | copy-start | bytes 3076
  0.0 4.9 %copy-start.1 = (bf16[512,256]{1,0:T(8,128)(2,1)S(1)}, bf16[512,256]{1,0:T(8,128)(2,1)}, u32[]{:S(2)}) copy-start(bf16[512,256]{1,0:T(8,128)(2,1)} %proj_ref.1) | copy-start | bytes 786436
  0.0 4.9 %copy-start.2 = (s32[512]{0:T(512)S(1)}, s32[512]{0:T(512)}, u32[]{:S(2)}) copy-start(s32[512]{0:T(512)} %param.8) | copy-start | bytes 6148
  0.0 5.0 %copy-start = (bf16[512,256]{1,0:T(8,128)(2,1)S(1)}, bf16[512,256]{1,0:T(8,128)(2,1)}, u32[]{:S(2)}) copy-start(bf16[512,256]{1,0:T(8,128)(2,1)} %feat_ref.1) | copy-start | bytes 786436
